TPU v7x, 32 devices: a whole 2x2x4 slice. The times are simulated.
32 devices in a mesh: dp: 4 (over y, core), expert: 2 (over x), group: 4 (over z).
Axes of the slice: x: 2, y: 2, z: 4, core: 2. Of those that a mesh axis runs over, the one named last changes fastest.
Arguments:
- tokens: bfloat16 [256, 7168], P(('dp', 'group')), may hold values from -6 to 6
- expert_ids: int32 [256, 8], P(('dp', 'group')), may hold values from 0 to 255, all different within a row; in each aligned block of 16 rows (0 to 15, 16 to 31, ...) at most 2 rows name the same one
- gate_values: bfloat16 [256, 8], P(('dp', 'group')), may hold values from 0.099609375 to 1
- gate_up: bfloat16 [2, 7168, 2, 2048], P('expert', None, None, 'group'), may hold values from -0.0625 to 0.0625
- down_weight: bfloat16 [2, 2048, 7168], P('expert', 'group'), may hold values from -0.125 to 0.125
- shared_gate_up: bfloat16 [7168, 2, 2048], P('expert', None, 'group'), may hold values from -0.0625 to 0.0625
- shared_down: bfloat16 [2048, 7168], P('group', 'expert'), may hold values from -0.125 to 0.125
Outputs:
- mixed: bfloat16 [256, 7168], P(('dp', 'group'), 'expert')
Inputs may be any that keep to these rules, and one draw needn't show every extreme that they name: `expert_ids`: each row names 8 different routed experts. In each aligned block of 16 rows (the rows of one device) no expert is named by more than 2 rows, and in some blocks one is named by exactly 2 rows.
All inputs are finite; a program needn't handle non-finite values.
Results may differ from a plain program's by a relative error of at most 0.028.
Values may be sent and summed in bfloat16 or wider, within the bound.
A program may use at most 128 MiB of HBM per device.

v0:
```python
import jax
import jax.numpy as jnp
from jax import lax
from jax.sharding import PartitionSpec as P


def expert_terms(block_tokens, block_weight, gate_up, down_weight):
    model_width = gate_up.shape[1]
    hidden_units = gate_up.shape[3]
    projected = jnp.dot(
        block_tokens,
        gate_up[0].reshape(model_width, 2 * hidden_units),
        preferred_element_type=jnp.float32,
    )
    gate_part = projected[:, :hidden_units]
    up_part = projected[:, hidden_units:]
    hidden = (jax.nn.silu(gate_part) * up_part).astype(jnp.bfloat16)
    product = jnp.dot(hidden, down_weight[0], preferred_element_type=jnp.float32)
    return (product * block_weight.astype(jnp.float32)[:, None]).astype(jnp.bfloat16)


def shared_block(token_columns, shared_gate_up, shared_down):
    column_width = shared_gate_up.shape[0]
    shared_units = shared_gate_up.shape[2]
    shared_partial = jnp.dot(
        token_columns,
        shared_gate_up.reshape(column_width, 2 * shared_units),
        preferred_element_type=jnp.float32,
    )
    shared_pre = lax.psum(shared_partial.astype(jnp.bfloat16), "expert").astype(jnp.float32)
    shared_hidden = (
        jax.nn.silu(shared_pre[:, :shared_units]) * shared_pre[:, shared_units:]
    ).astype(jnp.bfloat16)
    return jnp.dot(shared_hidden, shared_down, preferred_element_type=jnp.float32).astype(
        jnp.bfloat16
    )


def per_device(tokens, expert_ids, gate_values, gate_up, down_weight, shared_gate_up, shared_down):
    slot_index = lax.axis_index("expert")
    column_width = shared_gate_up.shape[0]
    chosen = expert_ids == slot_index
    weight_value = jnp.sum(
        jnp.where(chosen, gate_values.astype(jnp.float32), jnp.float32(0.0)), axis=1
    )
    slot_weight = weight_value.astype(jnp.bfloat16)
    gathered, gathered_weight = (
        lax.all_gather(tokens, "group", axis=0, tiled=True),
        lax.all_gather(slot_weight, "group", axis=0, tiled=True),
    )
    token_columns = lax.dynamic_slice_in_dim(gathered, slot_index * column_width, column_width, 1)
    shared_term = shared_block(token_columns, shared_gate_up, shared_down)
    partial_terms = expert_terms(gathered, gathered_weight, gate_up, down_weight)
    column_total = lax.psum_scatter(
        partial_terms, "expert", scatter_dimension=1, tiled=True
    ).astype(jnp.float32)
    mixed = lax.psum_scatter(
        (column_total + shared_term.astype(jnp.float32)).astype(jnp.bfloat16),
        "group",
        scatter_dimension=0,
        tiled=True,
    )
    return mixed


def solution(mesh):
    in_specs = (
        P(("dp", "group"), None),
        P(("dp", "group"), None),
        P(("dp", "group"), None),
        P("expert", None, None, "group"),
        P("expert", "group", None),
        P("expert", None, "group"),
        P("group", "expert"),
    )
    out_specs = P(("dp", "group"), "expert")
    return jax.shard_map(
        per_device, mesh=mesh, in_specs=in_specs, out_specs=out_specs, check_vma=False
    )
```

profile of v0, /device:TPU:0, one launch (start us, length us, event | category | flops | bytes accessed | tf_op | source)
XLA Modules:
  0.0 119.9 jit_solution(10707480298263581695)
XLA Ops:
  6.5 0.0 all-reduce.3.cloned.1.call-start
  6.5 23.4 %all_gather.6 = bf16[64,7168]{1,0:T(8,128)(2,1)} all-gather(bf16[16,7168]{1,0:T(8,128)(2,1)} %param.7), channel_id=1, replica_groups=mesh['dp'=4,'expert'=2,'group'=4] {'group'}, dimensions={0}, use_global_device_ids=true | all-gather | bytes 1146880 | tf_op jit(solution)/shard_map/all_gather | solution.py:48
  29.9 8.4 %copy.9 = bf16[448,8,2,512]{3,1,2,0:T(8,128)(2,1)} copy(bf16[448,8,2,512]{3,2,1,0:T(2,128)(2,1)} %bitcast.18) | data formatting | bytes 14680064
  38.3 5.4 %convolution_convert_fusion.1 = bf16[64,1024]{1,0:T(8,128)(2,1)} fusion(bf16[3584,1024]{1,0:T(8,128)(2,1)} %bitcast.14, bf16[64,7168]{1,0:T(8,128)(2,1)} %all_gather.6, s32[]{:T(128)S(6)} %select_n.8), kind=kOutput, calls=%fused_computation.7 | convolution fusion | flops 469827584 | bytes 7929860 | tf_op jit(solution)/shard_map/dot_general | solution.py:25
  43.7 0.0 all-reduce.3.cloned.1.call-update
  43.8 0.0 reduce-scatter.3.cloned.1.call-start
  43.8 0.0 copy-done.1
  43.8 0.0 copy-done.2
  43.9 0.0 copy-done.3
  43.9 0.6 dynamic-slice
  45.1 0.2 dynamic-update-slice
  45.4 10.1 %all-reduce = bf16[64]{0:T(256)(128)(2,1)S(1)} all-reduce(bf16[64]{0:T(256)(128)(2,1)S(1)} %dynamic-update-slice), channel_id=1, replica_groups=mesh['dp'=4,'expert'=2,'group'=4] {'group'}, use_global_device_ids=true, to_apply=%add | all-reduce | flops 64 | bytes 256
  55.5 0.0 slice-start.1
  55.5 10.4 %copy.8 = bf16[896,8,2,512]{3,1,2,0:T(8,128)(2,1)S(1)} copy(bf16[896,8,2,512]{3,2,1,0:T(2,128)(2,1)} %bitcast.17) | data formatting | bytes 29360128
  65.9 2.7 %fusion.15 = f32[64,1024]{1,0:T(8,128)S(1)} fusion(bf16[64,7168]{1,0:T(8,128)(2,1)S(1)} %copy-done, bf16[7168,1024]{1,0:T(8,128)(2,1)S(1)} %bitcast.13), kind=kOutput, calls=%fused_computation.19 | convolution fusion | flops 939524096 | bytes 15859712 | tf_op jit(solution)/shard_map/dot_general | solution.py:10
  68.7 2.3 %fusion = bf16[64,7168]{1,0:T(8,128)(2,1)} fusion(bf16[1,512,7168]{2,1,0:T(8,128)(2,1)S(1)} %bitcast.16, f32[64]{0:T(128)S(1)} %convert_element_type.39, f32[64,1024]{1,0:T(8,128)S(1)} %fusion.15), kind=kOutput, calls=%fused_computation.1 | convolution fusion | flops 470876160 | bytes 8519936 | tf_op jit(solution)/shard_map/dot_general | solution.py:18
  71.0 0.0 reduce-scatter.3.cloned.1.call-update
  71.0 0.0 reduce-scatter.5.cloned.1.call-start
  71.0 0.0 all-reduce.3.cloned.1.call-done
  71.1 0.9 convert_element_type.43
  72.0 16.3 %reduce-scatter.3.cloned.1.call-done = bf16[64,3584]{1,0:T(8,128)(2,1)} async-done(((bf16[64,7168]{1,0:T(8,128)(2,1)}), bf16[64,3584]{1,0:T(8,128)(2,1)}) %reduce-scatter.3.cloned.1.call-update) | async-done | bytes 458768 | tf_op jit(solution)/shard_map/reduce_scatter | solution.py:54
  88.3 3.6 %fusion.4 = bf16[64,3584]{1,0:T(8,128)(2,1)} fusion(bf16[512,3584]{1,0:T(8,128)(2,1)} %param.13, bf16[64,3584]{1,0:T(8,128)(2,1)} %reduce-scatter.3.cloned.1.call-done, f32[64,1024]{1,0:T(8,128)S(1)} %convert_element_type.43), kind=kOutput, calls=%fused_computation.6 | convolution fusion | flops 236224512 | bytes 4849664 | tf_op jit(solution)/shard_map/dot_general | solution.py:34
  91.9 0.0 reduce-scatter.5.cloned.1.call-update
  92.0 21.4 %reduce-scatter.5.cloned.1.call-done = bf16[16,3584]{1,0:T(8,128)(2,1)} async-done(((bf16[64,3584]{1,0:T(8,128)(2,1)}), bf16[16,3584]{1,0:T(8,128)(2,1)}) %reduce-scatter.5.cloned.1.call-update) | async-done | bytes 114704 | tf_op jit(solution)/shard_map/reduce_scatter | solution.py:57
  (12 shorter events, 0.0 us)
Async XLA Ops:
  6.5 64.5 %all-reduce.3.cloned.1.call-start = ((), (), s32[]{:S(2)}) async-start(), calls=%async_computation.3 | async-start | bytes 262144 | tf_op jit(solution)/shard_map/psum | solution.py:30
  38.3 5.5 %copy-start.1 = (s32[16,8]{0,1:T(8,128)S(1)}, s32[16,8]{0,1:T(8,128)}, u32[]{:S(2)}) copy-start(s32[16,8]{0,1:T(8,128)} %param.8) | copy-start | bytes 1540
  38.3 5.5 %copy-start.2 = (bf16[16,8]{0,1:T(8,128)(2,1)S(1)}, bf16[16,8]{0,1:T(8,128)(2,1)}, u32[]{:S(2)}) copy-start(bf16[16,8]{0,1:T(8,128)(2,1)} %param.9) | copy-start | bytes 772
  38.3 5.6 %copy-start.3 = (u32[32]{0:T(128)S(1)}, u32[32]{0:T(128)}, u32[]{:S(2)}) copy-start(u32[32]{0:T(128)} %constant.22) | copy-start | bytes 388
  38.3 30.3 %slice-start = ((s8[7340032]{0:T(1024)(128)(4,1)}), s8[3145728]{0:T(1024)(128)(4,1)S(1)}, s32[]{:S(2)}) async-start(s8[7340032]{0:T(1024)(128)(4,1)} %bitcast.15), calls=%async_computation.5 | async-start | bytes 6291456
  43.8 44.5 %reduce-scatter.3.cloned.1.call-start = ((), (), s32[]{:S(2)}) async-start(), calls=%async_computation.2 | async-start | bytes 1376256 | tf_op jit(solution)/shard_map/reduce_scatter | solution.py:54
  55.5 10.4 %copy-start = (bf16[64,7168]{1,0:T(8,128)(2,1)S(1)}, bf16[64,7168]{1,0:T(8,128)(2,1)}, u32[]{:S(2)}) copy-start(bf16[64,7168]{1,0:T(8,128)(2,1)} %all_gather.6) | copy-start | bytes 2752516
  55.5 13.1 %slice-start.1 = ((s8[7340032]{0:T(1024)(128)(4,1)}), s8[4194304]{0:T(1024)(128)(4,1)S(1)}, s32[]{:S(2)}) async-start(s8[7340032]{0:T(1024)(128)(4,1)} %bitcast.15), calls=%async_computation.6 | async-start | bytes 8388608
  71.0 42.4 %reduce-scatter.5.cloned.1.call-start = ((), (), s32[]{:S(2)}) async-start(), calls=%async_computation.4 | async-start | bytes 573440 | tf_op jit(solution)/shard_map/reduce_scatter | solution.py:57
Sparse Core Ops, SparseCore 0:
  43.9 20.9 all-reduce.2
  71.1 17.1 reduce-scatter.2
  92.1 21.2 reduce-scatter.4
where the time goes:
time: 120 us
  waiting for transfers between devices  37.8 us (31%)
  blocking collectives  33.5 us (28%)
  local copies, waits for them, and re-layouts  19.7 us (16%)
  matrix products  14.1 us (12%)
  between operations  13.9 us (12%)
    all_gather x1, blocking collectives, per_device(): lax.all_gather(tokens, 'group', axis=0, tiled=True)  23.4 us
    reduce_scatter x1, waiting for transfers between devices, per_device(): lax.psum_scatter((column_total + shared_term.astype(jnp.float32)).astype(...  21.4 us
    unnamed x17, local copies, waits for them, and re-layouts  19.7 us
    reduce_scatter x1, waiting for transfers between devices, per_device(): lax.psum_scatter(partial_terms, 'expert', scatter_dimension=1, tiled=True)  16.3 us
    unnamed x1, blocking collectives  10.1 us
    dot_general x1, matrix products, shared_block(): jnp.dot(token_columns, shared_gate_up.reshape(column_width, 2 * shared_un...  5.44 us
    dot_general x1, matrix products, shared_block(): jnp.dot(shared_hidden, shared_down, preferred_element_type=jnp.float32)  3.64 us
    dot_general x1, matrix products, expert_terms(): jnp.dot(block_tokens, gate_up[0].reshape(model_width, 2 * hidden_units),...  2.67 us
  transfers between devices with their start and end apart: 3, of which 2 were waited for; matrix products, arithmetic and copies ran while one was open for 14% of the time, Pallas kernels for 0%

commit v1 on v0

v1 whole, which is shorter than its diff:
```python
import functools

import jax
import jax.numpy as jnp
from jax import lax
from jax.experimental import pallas as pl
from jax.experimental.pallas import tpu as pltpu
from jax.sharding import PartitionSpec as P

MESH = pl.DeviceIdType.MESH
BF16, F32 = jnp.bfloat16, jnp.float32
CAP = 2
LANES = 128
DEPTH = 1792


def nearest_first(count):
    order = [0]
    for distance in range(1, count // 2 + 1):
        for candidate in (distance, count - distance):
            if candidate not in order:
                order.append(candidate)
    return order


def silu(value):
    return value / (1.0 + jnp.exp(-value))


def kernel(
    n_expert, n_group, batch,
    tokens, ids, gates, gate_up, down, shared_gate_up, shared_down,
    out,
    w_routed, w_down, w_shared, w_shared_down,
    x_all, x_shared, rows_all, x_routed,
    pre_own, pre_out, pre_in, term_out, term_in, routed_out, routed_in,
    routed_w_sem, down_w_sem, shared_w_sem, shared_down_w_sem, own_sem,
    x_send, x_recv, rows_send, rows_recv, pre_send, pre_recv,
    term_send, term_recv, routed_send, routed_recv,
):
    me_e, me_g = lax.axis_index("expert"), lax.axis_index("group")
    n_tokens, width = tokens.shape
    columns = x_all.shape[2]
    units = w_shared_down.shape[0]
    tiles = units // LANES
    pair = 2 if tiles % 2 == 0 else 1
    order = nearest_first(n_group)
    batches = [order[i : i + batch] for i in range(0, n_group, batch)]
    n_rows = batch * n_tokens

    def expert_at(distance):
        return lax.rem(me_e + n_expert + distance, n_expert)

    def group_at(distance):
        return lax.rem(me_g + n_group + distance, n_group)

    def weight_copies(source, target, sem):
        depth = min(DEPTH, source.shape[0])
        groups = []
        for n in range(source.shape[0] // depth):
            rows = pl.ds(n * depth, depth)
            groups.append([
                pltpu.make_async_copy(
                    source.at[rows, pl.ds(c * LANES, LANES)], target.at[c, rows], sem.at[n, c]
                )
                for c in range(tiles)
            ])
        return groups

    shared_groups = weight_copies(
        shared_gate_up.reshape(2 * columns, units), w_shared, shared_w_sem
    )
    routed_groups = weight_copies(gate_up.reshape(2 * width, units), w_routed, routed_w_sem)
    part = units // 4
    shared_down_copies = [
        pltpu.make_async_copy(
            shared_down.at[pl.ds(i * part, part)], w_shared_down.at[pl.ds(i * part, part)],
            shared_down_w_sem.at[i],
        )
        for i in range(4)
    ]
    down_copies = [
        pltpu.make_async_copy(
            down.at[0, :, pl.ds(pl.multiple_of(expert_at(-d) * columns, LANES), columns)],
            w_down.at[d],
            down_w_sem.at[d],
        )
        for d in range(n_expert)
    ]
    own_columns = pl.ds(pl.multiple_of(me_e * columns, LANES), columns)
    own_copy = pltpu.make_async_copy(tokens.at[:, own_columns], x_all.at[0], own_sem)
    own_copy.start()
    for group in shared_groups:
        for copy in group:
            copy.start()
    for copy in shared_down_copies:
        copy.start()
    for group in routed_groups:
        for copy in group:
            copy.start()
    for copy in down_copies:
        copy.start()

    barrier = pltpu.get_barrier_semaphore()
    for d in range(n_expert):
        for s in range(n_group):
            if d or s:
                pl.semaphore_signal(
                    barrier, inc=1,
                    device_id={"expert": expert_at(d), "group": group_at(s)},
                    device_id_type=MESH,
                )

    before = (
        lax.broadcasted_iota(jnp.int32, (n_tokens, n_tokens), 0)
        < lax.broadcasted_iota(jnp.int32, (n_tokens, n_tokens), 1)
    ).astype(BF16)
    ranks = lax.broadcasted_iota(jnp.int32, (8, n_tokens), 0).astype(F32)

    def picked_by(expert):
        chosen = ids[...] == expert
        named = jnp.sum(jnp.where(chosen, 1.0, 0.0), axis=0, keepdims=True)
        value = jnp.sum(jnp.where(chosen, gates[...].astype(F32), 0.0), axis=0, keepdims=True)
        named = jnp.broadcast_to(named, (8, n_tokens))
        rank = jnp.dot(named.astype(BF16), before, preferred_element_type=F32)
        picked = jnp.where((named > 0.5) & (jnp.abs(rank - ranks) < 0.5), 1.0, 0.0)
        return picked, jnp.broadcast_to(value, (8, n_tokens))

    picked, _ = picked_by(me_e)
    selected = jnp.dot(picked.astype(BF16), tokens[...], preferred_element_type=F32)
    rows_all[0] = selected[:CAP].astype(BF16)

    pl.semaphore_wait(barrier, n_expert * n_group - 1)

    x_copies, rows_copies = {}, {}
    for s in order[1:]:
        x_copies[s] = pltpu.make_async_remote_copy(
            src_ref=tokens.at[:, own_columns], dst_ref=x_all.at[s],
            send_sem=x_send.at[s], recv_sem=x_recv.at[s],
            device_id={"group": group_at(s)}, device_id_type=MESH,
        )
        x_copies[s].start()
    for s in order[1:]:
        rows_copies[s] = pltpu.make_async_remote_copy(
            src_ref=rows_all.at[0], dst_ref=rows_all.at[s],
            send_sem=rows_send.at[s], recv_sem=rows_recv.at[s],
            device_id={"group": group_at(s)}, device_id_type=MESH,
        )
        rows_copies[s].start()

    feature = lax.broadcasted_iota(jnp.int32, (LANES, 4 * LANES), 0)
    place = lax.broadcasted_iota(jnp.int32, (LANES, 4 * LANES), 1)
    spread = (
        (place == 2 * feature) | (place == 2 * feature + 1 + 2 * LANES)
    ).astype(BF16)

    def project(x, weights, groups, wait):
        depth = min(DEPTH, x.shape[1])
        totals = [None] * (tiles // pair)
        for n in range(x.shape[1] // depth):
            if wait:
                for copy in groups[n]:
                    copy.wait()
            rows = pl.ds(n * depth, depth)
            x_part = x[:, n * depth : (n + 1) * depth]
            for p in range(tiles // pair):
                block = [weights[p * pair + i, rows] for i in range(pair)]
                block = jnp.concatenate(block, axis=1) if pair > 1 else block[0]
                product = jnp.dot(x_part, block, preferred_element_type=F32)
                totals[p] = product if totals[p] is None else totals[p] + product
        return totals

    pre_copies = []
    for b, members in enumerate(batches):
        for s in members:
            if s:
                x_copies[s].wait_recv()
            else:
                own_copy.wait()

        def expand(j, carry, members=members):
            source = pl.ds(pl.multiple_of(j * LANES, LANES), LANES)
            target = pl.ds(pl.multiple_of(j * 2 * LANES, 2 * LANES), 2 * LANES)
            part = jnp.concatenate([x_all[s, :, source] for s in members], axis=0)
            both = jnp.dot(part, spread, preferred_element_type=F32).astype(BF16)
            x_shared[:n_rows, target] = both[:, : 2 * LANES]
            x_shared[n_rows:, target] = both[:, 2 * LANES :]
            return carry

        lax.fori_loop(0, columns // LANES, expand, 0, unroll=True)
        for p, total in enumerate(project(x_shared, w_shared, shared_groups, b == 0)):
            at = pl.ds(p * pair * LANES, pair * LANES)
            pre_own[b, :, at] = total
            pre_out[b, :, at] = total.astype(BF16)
        copies = []
        for d in range(1, n_expert):
            copy = pltpu.make_async_remote_copy(
                src_ref=pre_out.at[b], dst_ref=pre_in.at[d - 1, b],
                send_sem=pre_send.at[d - 1, b], recv_sem=pre_recv.at[d - 1, b],
                device_id={"expert": expert_at(d)}, device_id_type=MESH,
            )
            copy.start()
            copies.append(copy)
        pre_copies.append(copies)

    term_copies = {}
    piece = columns // 7 if columns % (7 * LANES) == 0 else columns
    for b, members in enumerate(batches):
        for copy in pre_copies[b]:
            copy.wait_recv()
        total = pre_own[b]
        for d in range(1, n_expert):
            total = total + pre_in[d - 1, b].astype(F32)
        hidden = (silu(total[:n_rows]) * total[n_rows:]).astype(BF16)
        if b == 0:
            for copy in shared_down_copies:
                copy.wait()
        for n in range(columns // piece):
            at = pl.ds(n * piece, piece)
            term = jnp.dot(hidden, w_shared_down[:, at], preferred_element_type=F32).astype(BF16)
            for i, s in enumerate(members):
                rows = term[i * n_tokens : (i + 1) * n_tokens]
                if s:
                    term_out[s, :, at] = rows
                else:
                    term_in[0, :, at] = rows
        for s in members:
            if s:
                term_copies[s] = pltpu.make_async_remote_copy(
                    src_ref=term_out.at[s], dst_ref=term_in.at[s],
                    send_sem=term_send.at[s], recv_sem=term_recv.at[s],
                    device_id={"group": group_at(-s)}, device_id_type=MESH,
                )
                term_copies[s].start()

    for s in order[1:]:
        rows_copies[s].wait_recv()
    routed_rows = n_group * CAP

    def expand_rows(j, carry):
        source = pl.ds(pl.multiple_of(j * LANES, LANES), LANES)
        target = pl.ds(pl.multiple_of(j * 2 * LANES, 2 * LANES), 2 * LANES)
        part = rows_all[:, :, source].reshape(routed_rows, LANES)
        both = jnp.dot(part, spread, preferred_element_type=F32).astype(BF16)
        x_routed[:routed_rows, target] = both[:, : 2 * LANES]
        x_routed[routed_rows:, target] = both[:, 2 * LANES :]
        return carry

    lax.fori_loop(0, width // LANES, expand_rows, 0, unroll=True)
    totals = project(x_routed, w_routed, routed_groups, True)
    hidden = jnp.concatenate(
        [(silu(t[:routed_rows]) * t[routed_rows:]).astype(BF16) for t in totals], axis=1
    )
    routed_copies = {}
    for d in reversed(range(n_expert)):
        down_copies[d].wait()
        for n in range(columns // piece):
            at = pl.ds(n * piece, piece)
            term = jnp.dot(hidden, w_down[d, :, at], preferred_element_type=F32).astype(BF16)
            for s in range(n_group):
                rows = term[s * CAP : (s + 1) * CAP]
                if d or s:
                    routed_out[d, s, :, at] = rows
                else:
                    routed_in[0, 0, :, at] = rows
        for s in order:
            if d or s:
                routed_copies[d, s] = pltpu.make_async_remote_copy(
                    src_ref=routed_out.at[d, s], dst_ref=routed_in.at[d, s],
                    send_sem=routed_send.at[d, s], recv_sem=routed_recv.at[d, s],
                    device_id={"expert": expert_at(-d), "group": group_at(-s)},
                    device_id_type=MESH,
                )
                routed_copies[d, s].start()

    identity = (
        lax.broadcasted_iota(jnp.int32, (n_tokens, n_tokens), 0)
        == lax.broadcasted_iota(jnp.int32, (n_tokens, n_tokens), 1)
    ).astype(BF16)
    weights = []
    for d in range(n_expert):
        picked, value = picked_by(expert_at(d))
        weights.append(lax.dot_general(
            identity, (picked * value).astype(BF16), (((1,), (1,)), ((), ())),
            preferred_element_type=F32,
        ))
    for s in order[1:]:
        term_copies[s].wait_recv()
    for copy in routed_copies.values():
        copy.wait_recv()
    for n in range(columns // piece):
        at = pl.ds(n * piece, piece)
        total = term_in[0, :, at].astype(F32)
        for s in order[1:]:
            total = total + term_in[s, :, at].astype(F32)
        for d in range(n_expert):
            rows = routed_in[d, 0, :, at].astype(F32)
            for s in range(1, n_group):
                rows = rows + routed_in[d, s, :, at].astype(F32)
            for r in range(CAP):
                total = total + weights[d][:, r : r + 1] * rows[r : r + 1]
        out[:, at] = total.astype(BF16)

    for copies in (x_copies, rows_copies, term_copies, routed_copies):
        for copy in copies.values():
            copy.wait_send()
    for copies in pre_copies:
        for copy in copies:
            copy.wait_send()


def per_device(n_expert, n_group, tokens, ids, gates, gate_up, down, shared_gate_up, shared_down):
    n_tokens, width = tokens.shape
    columns, _, units = shared_gate_up.shape
    tiles = units // LANES
    batch = 2 if n_group % 2 == 0 else 1
    n_batches = n_group // batch
    n_rows = batch * n_tokens
    vmem, dma = pltpu.VMEM, pltpu.SemaphoreType.DMA
    in_vmem, in_hbm = pl.BlockSpec(memory_space=pltpu.VMEM), pl.BlockSpec(memory_space=pltpu.HBM)
    return pl.pallas_call(
        functools.partial(kernel, n_expert, n_group, batch),
        out_shape=jax.ShapeDtypeStruct((n_tokens, columns), BF16),
        in_specs=[in_vmem] * 3 + [in_hbm] * 4,
        out_specs=in_vmem,
        scratch_shapes=[
            vmem((tiles, 2 * width, LANES), BF16),
            vmem((n_expert, units, columns), BF16),
            vmem((tiles, 2 * columns, LANES), BF16),
            vmem((units, columns), BF16),
            vmem((n_group, n_tokens, columns), BF16),
            vmem((2 * n_rows, 2 * columns), BF16),
            vmem((n_group, CAP, width), BF16),
            vmem((2 * n_group * CAP, 2 * width), BF16),
            vmem((n_batches, 2 * n_rows, units), F32),
            vmem((n_batches, 2 * n_rows, units), BF16),
            vmem((max(1, n_expert - 1), n_batches, 2 * n_rows, units), BF16),
            vmem((n_group, n_tokens, columns), BF16),
            vmem((n_group, n_tokens, columns), BF16),
            vmem((n_expert, n_group, CAP, columns), BF16),
            vmem((n_expert, n_group, CAP, columns), BF16),
            dma((max(1, 2 * width // DEPTH), tiles)),
            dma((n_expert,)),
            dma((max(1, 2 * columns // DEPTH), tiles)),
            dma((4,)),
            dma,
            dma((n_group,)), dma((n_group,)),
            dma((n_group,)), dma((n_group,)),
            dma((max(1, n_expert - 1), n_batches)), dma((max(1, n_expert - 1), n_batches)),
            dma((n_group,)), dma((n_group,)),
            dma((n_expert, n_group)), dma((n_expert, n_group)),
        ],
        compiler_params=pltpu.CompilerParams(
            collective_id=0, has_side_effects=True, vmem_limit_bytes=60 * 2**20
        ),
    )(tokens, ids.T, gates.T, gate_up, down, shared_gate_up, shared_down)


def solution(mesh):
    in_specs = (
        P(("dp", "group"), None),
        P(("dp", "group"), None),
        P(("dp", "group"), None),
        P("expert", None, None, "group"),
        P("expert", "group", None),
        P("expert", None, "group"),
        P("group", "expert"),
    )
    return jax.shard_map(
        functools.partial(per_device, mesh.shape["expert"], mesh.shape["group"]),
        mesh=mesh, in_specs=in_specs, out_specs=P(("dp", "group"), "expert"), check_vma=False,
    )
```

time: 120 us -> 38 us (0.32)
  waiting for transfers between devices: 37.8 us -> 0 us
  Pallas kernels: 0 us -> 36.3 us
  blocking collectives: 33.5 us -> 0 us
  local copies, waits for them, and re-layouts: 19.7 us -> 1.55 us
  matrix products: 14.1 us -> 0 us
  between operations: 13.9 us -> 0.01 us
    reduce_scatter x2 -> x0, waiting for transfers between devices: 37.7 us -> none  [the longest x1 21.4 us: per_device(): lax.psum_scatter((column_total + shared_term.astype(jnp.float32)).astype(...]
    pallas_call x0 -> x1, Pallas kernels: none -> 36.3 us  [per_device(): pl.pallas_call(functools.partial(kernel, n_expert, n_group, batch), out_s...]
    all_gather x1 -> x0, blocking collectives: 23.4 us -> none  [per_device(): lax.all_gather(tokens, 'group', axis=0, tiled=True)]
    unnamed x17 -> x1, local copies, waits for them, and re-layouts: 19.7 us -> 1.55 us
    dot_general x4 -> x0, matrix products: 14.1 us -> none  [the longest x1 5.44 us: shared_block(): jnp.dot(token_columns, shared_gate_up.reshape(column_width, 2 * shared_un...]
    unnamed x1 -> x0, blocking collectives: 10.1 us -> none
  transfers between devices with their start and end apart: 3 -> 0, of which waited for: 2 -> 0; matrix products, arithmetic and copies ran while one was open for 14% -> 0% of each run, Pallas kernels for 0% -> 0%
where the time goes in v1:
time: 38 us; the launch traced here: 37.8 us
  Pallas kernels  36.3 us (96%)
  local copies, waits for them, and re-layouts  1.55 us (4%)
    pallas_call x1, Pallas kernels, per_device(): pl.pallas_call(functools.partial(kernel, n_expert, n_group, batch), out_s...  36.3 us
    unnamed x1, local copies, waits for them, and re-layouts  1.55 us

profile of v1, /device:TPU:0, one launch (start us, length us, event | category | flops | bytes accessed | tf_op | source)
XLA Modules:
  0.0 37.8 jit_solution(14594786789018383544)
XLA Ops:
  0.0 36.3 %shard_map.73 = bf16[16,3584]{1,0:T(8,128)(2,1)} custom-call(bf16[16,7168]{1,0:T(8,128)(2,1)} %tokens.1, s32[8,16]{1,0:T(8,128)} %bitcast.2, bf16[8,16]{1,0:T(8,128)(2,1)} %bitcast.3, bf16[1,7168,2,512]{3,2,1,0:T(2,128)(2,1)} %gate_up.1, bf16[1,512,7168]{2,1,0:T(8,128)(2,1)} %down.1, bf16[3584,2,512]{2,1,0:T(2,128)(2,1)} %shared_gate_up.1, ...), custom_call_target="tpu_custom_call" | custom-call | tf_op jit(solution)/shard_map/pallas_call | solution.py:321
  36.3 1.6 %copy.9 = bf16[16,3584]{1,0:T(8,128)(2,1)} copy(bf16[16,3584]{1,0:T(8,128)(2,1)} %shard_map.73) | data formatting | bytes 229376

commit v2 on v1

--- a/solution.py
+++ b/solution.py
@@ -15,7 +15,7 @@
 
 
 def nearest_first(count):
-    order = [0]
+    order = []
     for distance in range(1, count // 2 + 1):
         for candidate in (distance, count - distance):
             if candidate not in order:
@@ -23,12 +23,21 @@
     return order
 
 
+def batches_of(count):
+    order = nearest_first(count) + [0]
+    return [order[i : i + 2] for i in range(0, count, 2)]
+
+
+def schedule_of(batches):
+    return [(kind, b) for kind in ("pre", "fin") for b in range(len(batches))]
+
+
 def silu(value):
     return value / (1.0 + jnp.exp(-value))
 
 
 def kernel(
-    n_expert, n_group, batch,
+    n_expert, n_group,
     tokens, ids, gates, gate_up, down, shared_gate_up, shared_down,
     out,
     w_routed, w_down, w_shared, w_shared_down,
@@ -45,8 +54,7 @@
     tiles = units // LANES
     pair = 2 if tiles % 2 == 0 else 1
     order = nearest_first(n_group)
-    batches = [order[i : i + batch] for i in range(0, n_group, batch)]
-    n_rows = batch * n_tokens
+    batches = batches_of(n_group)
 
     def expert_at(distance):
         return lax.rem(me_e + n_expert + distance, n_expert)
@@ -133,14 +141,30 @@
     pl.semaphore_wait(barrier, n_expert * n_group - 1)
 
     x_copies, rows_copies = {}, {}
-    for s in order[1:]:
+    relayed = n_group == 4
+    for s in [1, 3] if relayed else order:
         x_copies[s] = pltpu.make_async_remote_copy(
             src_ref=tokens.at[:, own_columns], dst_ref=x_all.at[s],
             send_sem=x_send.at[s], recv_sem=x_recv.at[s],
             device_id={"group": group_at(s)}, device_id_type=MESH,
         )
         x_copies[s].start()
-    for s in order[1:]:
+    x_arrivals = {s: [copy] for s, copy in x_copies.items()}
+    if relayed:
+        half = columns // 2
+        for s, sem, first in ((1, 2, 0), (3, 0, half)):
+            x_copies[s].wait_recv()
+            at = pl.ds(first, half)
+            relay = pltpu.make_async_remote_copy(
+                src_ref=x_all.at[s, :, at], dst_ref=x_all.at[2, :, at],
+                send_sem=x_send.at[sem], recv_sem=x_recv.at[sem],
+                device_id={"group": group_at(s)}, device_id_type=MESH,
+            )
+            relay.start()
+            x_arrivals[s] = []
+            x_arrivals.setdefault(2, []).append(relay)
+            x_copies["relay", s] = relay
+    for s in order:
         rows_copies[s] = pltpu.make_async_remote_copy(
             src_ref=rows_all.at[0], dst_ref=rows_all.at[s],
             send_sem=rows_send.at[s], recv_sem=rows_recv.at[s],
@@ -162,7 +186,7 @@
                 for copy in groups[n]:
                     copy.wait()
             rows = pl.ds(n * depth, depth)
-            x_part = x[:, n * depth : (n + 1) * depth]
+            x_part = x[:, pl.ds(n * depth, depth)]
             for p in range(tiles // pair):
                 block = [weights[p * pair + i, rows] for i in range(pair)]
                 block = jnp.concatenate(block, axis=1) if pair > 1 else block[0]
@@ -170,51 +194,61 @@
                 totals[p] = product if totals[p] is None else totals[p] + product
         return totals
 
-    pre_copies = []
-    for b, members in enumerate(batches):
+    pre_copies, term_copies = {}, {}
+    piece = columns // 7 if columns % (7 * LANES) == 0 else columns
+    shared_waits = list(shared_groups)
+
+    def pre(b):
+        members = batches[b]
+        n_rows = len(members) * n_tokens
         for s in members:
             if s:
-                x_copies[s].wait_recv()
+                for copy in x_arrivals[s]:
+                    copy.wait_recv()
             else:
                 own_copy.wait()
 
-        def expand(j, carry, members=members):
+        def expand(j, carry):
             source = pl.ds(pl.multiple_of(j * LANES, LANES), LANES)
             target = pl.ds(pl.multiple_of(j * 2 * LANES, 2 * LANES), 2 * LANES)
             part = jnp.concatenate([x_all[s, :, source] for s in members], axis=0)
             both = jnp.dot(part, spread, preferred_element_type=F32).astype(BF16)
             x_shared[:n_rows, target] = both[:, : 2 * LANES]
-            x_shared[n_rows:, target] = both[:, 2 * LANES :]
+            x_shared[n_rows : 2 * n_rows, target] = both[:, 2 * LANES :]
             return carry
 
         lax.fori_loop(0, columns // LANES, expand, 0, unroll=True)
-        for p, total in enumerate(project(x_shared, w_shared, shared_groups, b == 0)):
+        totals = project(x_shared.at[: 2 * n_rows], w_shared, shared_groups, bool(shared_waits))
+        shared_waits.clear()
+        for p, total in enumerate(totals):
             at = pl.ds(p * pair * LANES, pair * LANES)
-            pre_own[b, :, at] = total
-            pre_out[b, :, at] = total.astype(BF16)
-        copies = []
+            pre_own[b, : 2 * n_rows, at] = total
+            pre_out[b, : 2 * n_rows, at] = total.astype(BF16)
+        pre_copies[b] = []
         for d in range(1, n_expert):
+            rows = pl.ds(0, 2 * n_rows)
             copy = pltpu.make_async_remote_copy(
-                src_ref=pre_out.at[b], dst_ref=pre_in.at[d - 1, b],
+                src_ref=pre_out.at[b, rows], dst_ref=pre_in.at[d - 1, b, rows],
                 send_sem=pre_send.at[d - 1, b], recv_sem=pre_recv.at[d - 1, b],
                 device_id={"expert": expert_at(d)}, device_id_type=MESH,
             )
             copy.start()
-            copies.append(copy)
-        pre_copies.append(copies)
-
-    term_copies = {}
-    piece = columns // 7 if columns % (7 * LANES) == 0 else columns
-    for b, members in enumerate(batches):
+            pre_copies[b].append(copy)
+
+    down_waits = list(shared_down_copies)
+
+    def fin(b):
+        members = batches[b]
+        n_rows = len(members) * n_tokens
         for copy in pre_copies[b]:
             copy.wait_recv()
-        total = pre_own[b]
+        total = pre_own[b, : 2 * n_rows]
         for d in range(1, n_expert):
-            total = total + pre_in[d - 1, b].astype(F32)
+            total = total + pre_in[d - 1, b, : 2 * n_rows].astype(F32)
         hidden = (silu(total[:n_rows]) * total[n_rows:]).astype(BF16)
-        if b == 0:
-            for copy in shared_down_copies:
-                copy.wait()
+        for copy in down_waits:
+            copy.wait()
+        down_waits.clear()
         for n in range(columns // piece):
             at = pl.ds(n * piece, piece)
             term = jnp.dot(hidden, w_shared_down[:, at], preferred_element_type=F32).astype(BF16)
@@ -233,7 +267,10 @@
                 )
                 term_copies[s].start()
 
-    for s in order[1:]:
+    for kind, b in schedule_of(batches):
+        (pre if kind == "pre" else fin)(b)
+
+    for s in order:
         rows_copies[s].wait_recv()
     routed_rows = n_group * CAP
 
@@ -263,7 +300,7 @@
                     routed_out[d, s, :, at] = rows
                 else:
                     routed_in[0, 0, :, at] = rows
-        for s in order:
+        for s in order + [0]:
             if d or s:
                 routed_copies[d, s] = pltpu.make_async_remote_copy(
                     src_ref=routed_out.at[d, s], dst_ref=routed_in.at[d, s],
@@ -284,14 +321,14 @@
             identity, (picked * value).astype(BF16), (((1,), (1,)), ((), ())),
             preferred_element_type=F32,
         ))
-    for s in order[1:]:
+    for s in order:
         term_copies[s].wait_recv()
     for copy in routed_copies.values():
         copy.wait_recv()
     for n in range(columns // piece):
         at = pl.ds(n * piece, piece)
         total = term_in[0, :, at].astype(F32)
-        for s in order[1:]:
+        for s in order:
             total = total + term_in[s, :, at].astype(F32)
         for d in range(n_expert):
             rows = routed_in[d, 0, :, at].astype(F32)
@@ -304,7 +341,7 @@
     for copies in (x_copies, rows_copies, term_copies, routed_copies):
         for copy in copies.values():
             copy.wait_send()
-    for copies in pre_copies:
+    for copies in pre_copies.values():
         for copy in copies:
             copy.wait_send()
 
@@ -313,13 +350,13 @@
     n_tokens, width = tokens.shape
     columns, _, units = shared_gate_up.shape
     tiles = units // LANES
-    batch = 2 if n_group % 2 == 0 else 1
-    n_batches = n_group // batch
-    n_rows = batch * n_tokens
+    batches = batches_of(n_group)
+    n_batches = len(batches)
+    n_rows = max(len(members) for members in batches) * n_tokens
     vmem, dma = pltpu.VMEM, pltpu.SemaphoreType.DMA
     in_vmem, in_hbm = pl.BlockSpec(memory_space=pltpu.VMEM), pl.BlockSpec(memory_space=pltpu.HBM)
     return pl.pallas_call(
-        functools.partial(kernel, n_expert, n_group, batch),
+        functools.partial(kernel, n_expert, n_group),
         out_shape=jax.ShapeDtypeStruct((n_tokens, columns), BF16),
         in_specs=[in_vmem] * 3 + [in_hbm] * 4,
         out_specs=in_vmem,

time: 38 us -> 37.6 us (0.989)
  Pallas kernels: 36.3 us -> 35.9 us
where the time goes in v2:
time: 37.6 us; the launch traced here: 37.5 us
  Pallas kernels  35.9 us (95%)
  local copies, waits for them, and re-layouts  1.55 us (4%)
    pallas_call x1, Pallas kernels, per_device(): pl.pallas_call(functools.partial(kernel, n_expert, n_group), out_shape=ja...  35.9 us
    unnamed x1, local copies, waits for them, and re-layouts  1.55 us

profile of v2, /device:TPU:0, one launch (start us, length us, event | category | flops | bytes accessed | tf_op | source)
XLA Modules:
  0.0 37.5 jit_solution(10662949284057846283)
XLA Ops:
  0.0 35.9 %shard_map.73 = bf16[16,3584]{1,0:T(8,128)(2,1)} custom-call(bf16[16,7168]{1,0:T(8,128)(2,1)} %tokens.1, s32[8,16]{1,0:T(8,128)} %bitcast.2, bf16[8,16]{1,0:T(8,128)(2,1)} %bitcast.3, bf16[1,7168,2,512]{3,2,1,0:T(2,128)(2,1)} %gate_up.1, bf16[1,512,7168]{2,1,0:T(8,128)(2,1)} %down.1, bf16[3584,2,512]{2,1,0:T(2,128)(2,1)} %shared_gate_up.1, ...), custom_call_target="tpu_custom_call" | custom-call | tf_op jit(solution)/shard_map/pallas_call | solution.py:358
  35.9 1.6 %copy.9 = bf16[16,3584]{1,0:T(8,128)(2,1)} copy(bf16[16,3584]{1,0:T(8,128)(2,1)} %shard_map.73) | data formatting | bytes 229376
